TPU v7x, 32 devices: a whole 2x2x4 slice. The times are simulated.
32 devices in a mesh: dp: 8 (over z, x), seq: 4 (over y, core).
Axes of the slice: x: 2, y: 2, z: 4, core: 2. Of those that a mesh axis runs over, the one named last changes fastest.
Arguments:
- x_long: bfloat16 [32, 640, 768], P('dp', 'seq'), may hold values from -6 to 6
- x_short: bfloat16 [64, 160, 768], P(('dp', 'seq')), may hold values from -6 to 6
- seg_long: int32 [32, 640], P('dp'), may hold values from 0 to 4, never falling along the last dimension, each value on 1 to 256 neighbouring positions
- seg_short: int32 [64, 160], P(('dp', 'seq')), may hold values from 0 to 2, never falling along the last dimension, each value on 1 to 80 neighbouring positions
- pred_long: int32 [32, 640], P('dp', 'seq'), may hold values from 0 to 23
- target_long: int32 [32, 640], P('dp', 'seq'), may hold values from 0 to 23
- pred_short: int32 [64, 160], P(('dp', 'seq')), may hold values from 0 to 23
- target_short: int32 [64, 160], P(('dp', 'seq')), may hold values from 0 to 23
- query_weight: bfloat16 [768, 768], replicated, may hold values from -0.21875 to 0.21875
- key_weight: bfloat16 [768, 768], replicated, may hold values from -0.21875 to 0.21875
- value_weight: bfloat16 [768, 768], replicated, may hold values from -0.21875 to 0.21875
- out_weight: bfloat16 [768, 768], replicated, may hold values from -1.75 to 1.75
- up_weight: bfloat16 [768, 3072], replicated, may hold values from -0.21875 to 0.21875
- down_weight: bfloat16 [3072, 768], replicated, may hold values from -0.109375 to 0.109375
- vectors: float32 [8, 768], replicated, may hold values from -2.5 to 2.5, as said below
- up_bias: float32 [3072], replicated, may hold values from -3 to 3
- grad_long: bfloat16 [32, 640, 768], P(('dp', 'seq')), may hold values from -6 to 6
- grad_short: bfloat16 [64, 160, 768], P(('dp', 'seq')), may hold values from -6 to 6
Outputs:
- out_long: float32 [32, 640, 768], P(('dp', 'seq'))
- out_short: float32 [64, 160, 768], P(('dp', 'seq'))
- back_long: float32 [32, 640, 768], P('dp', 'seq')
- back_short: float32 [64, 160, 768], P(('dp', 'seq'))
- query_grad: float32 [768, 768], replicated
- key_grad: float32 [768, 768], replicated
- value_grad: float32 [768, 768], replicated
- out_grad: float32 [768, 768], replicated
- up_grad: float32 [768, 3072], replicated
- down_grad: float32 [3072, 768], replicated
- vector_grad: float32 [8, 768], replicated
- bias_grad: float32 [3072], replicated
- residue_counts: int32 [3, 24], replicated
Inputs may be any that keep to these rules, and one draw needn't show every extreme that they name: `seg_long`: segment 0 is padding at the start of a row; other numbers are packed chains. `seg_short`: segment 0 is padding at the start of a row; other numbers are packed chains. `vectors`: rows 4 and 6 are norm gains near one; the others are biases and shifts.
All inputs are finite; a program needn't handle non-finite values.
Results may differ from a plain program's by a relative error of at most 0.02.
Values may be sent and summed in bfloat16 or wider, within the bound.
A program may use at most 256 MiB of HBM per device.

v0:
```python
import jax
import jax.numpy as jnp
from jax import lax
from jax.sharding import PartitionSpec as P

HEADS = 12
VOCAB = 24


epsilon = 1e-05
blocked = -1e30


def project(matrix, weight):
    return jnp.dot(matrix, weight, preferred_element_type=jnp.float32)


def outer_sum(first_op, second_op):
    return lax.dot_general(
        first_op, second_op, (((0,), (0,)), ((), ())), preferred_element_type=jnp.float32
    )


def against(matrix, weight):
    return lax.dot_general(
        matrix, weight, (((1,), (1,)), ((), ())), preferred_element_type=jnp.float32
    )


def normalize(residual, gain_row, shift_row):
    centered = residual - jnp.mean(residual, -1, keepdims=True)
    factor = lax.rsqrt(jnp.mean(centered * centered, -1, keepdims=True) + epsilon)
    normed = centered * factor
    return (normed * gain_row + shift_row, normed, factor)


def normalize_back(upward, normed, factor, gain_row):
    scaled = upward * gain_row
    result = factor * (
        scaled
        - jnp.mean(scaled, -1, keepdims=True)
        - normed * jnp.mean(scaled * normed, -1, keepdims=True)
    )
    return (result, jnp.sum(upward * normed, 0), jnp.sum(upward, 0))


def visible(seg_query, seg_keys):
    return (seg_query[:, :, None] == seg_keys[:, None, :])[:, None]


def raw_scores(queries, keys_in):
    factor = queries.shape[-1] ** (-0.5)
    return (
        jnp.einsum("rqhe,rkhe->rhqk", queries, keys_in, preferred_element_type=jnp.float32) * factor
    )


def attend(queries, keys_in, values_in, seg_query, seg_keys):
    allowed = visible(seg_query, seg_keys)
    scores = jnp.where(allowed, raw_scores(queries, keys_in), blocked)
    highest = jnp.max(scores, -1, keepdims=True)
    weights = jnp.where(allowed, jnp.exp(scores - highest), 0.0)
    summed = jnp.sum(weights, -1, keepdims=True)
    mixture = jnp.einsum(
        "rhqk,rkhe->rqhe",
        weights / summed,
        values_in.astype(jnp.float32),
        preferred_element_type=jnp.float32,
    )
    return (mixture, (highest + jnp.log(summed))[..., 0])


def fold_attend(query_long, local_pair, seg_local, seg_long):
    batch_rows, query_count, head_count, head_size = query_long.shape
    pieces = (
        lax.all_gather(local_pair[0], "seq", axis=1, tiled=True),
        lax.all_gather(local_pair[1], "seq", axis=1, tiled=True),
    )
    running_max = jnp.full((batch_rows, head_count, query_count), blocked, jnp.float32)
    piece_len = pieces[0].shape[1]
    keys_piece = pieces[0].reshape(batch_rows, piece_len, head_count, head_size)
    values_piece = (
        pieces[1].reshape(batch_rows, piece_len, head_count, head_size).astype(jnp.float32)
    )
    allowed = visible(seg_local, seg_long)
    scores = jnp.where(allowed, raw_scores(query_long, keys_piece), blocked)
    new_max = jnp.maximum(running_max, jnp.max(scores, -1))
    weights = jnp.where(allowed, jnp.exp(scores - new_max[..., None]), 0.0)
    running_sum = jnp.sum(weights, -1)
    running_acc = jnp.einsum(
        "rhqk,rkhe->rhqe", weights, values_piece, preferred_element_type=jnp.float32
    )
    mixture = jnp.transpose(running_acc / running_sum[..., None], (0, 2, 1, 3))
    return (mixture, new_max + jnp.log(running_sum))


def attend_back(queries, keys_in, values_in, seg_query, seg_keys, logsum, mixture_grad):
    factor = queries.shape[-1] ** (-0.5)
    allowed = visible(seg_query, seg_keys)
    weights = jnp.where(allowed, jnp.exp(raw_scores(queries, keys_in) - logsum[..., None]), 0.0)
    weight_grad = jnp.einsum(
        "rqhe,rkhe->rhqk", mixture_grad, values_in, preferred_element_type=jnp.float32
    )
    score_grad = (
        weights * (weight_grad - jnp.sum(weights * weight_grad, -1, keepdims=True))
    ).astype(jnp.bfloat16)
    query_part = (
        jnp.einsum("rhqk,rkhe->rqhe", score_grad, keys_in, preferred_element_type=jnp.float32)
        * factor
    )
    key_part = (
        jnp.einsum("rhqk,rqhe->rkhe", score_grad, queries, preferred_element_type=jnp.float32)
        * factor
    )
    value_part = jnp.einsum(
        "rhqk,rqhe->rkhe",
        weights,
        mixture_grad.astype(jnp.float32),
        preferred_element_type=jnp.float32,
    )
    return (query_part, key_part, value_part)


def tally(predicted, target, segment):
    residues = jnp.arange(VOCAB, dtype=jnp.int32)[None, :]
    live_mask = (segment > 0).reshape(-1, 1)
    predicted = predicted.reshape(-1, 1)
    target = target.reshape(-1, 1)
    predicted_hot = (predicted == residues) & live_mask
    target_hot = (target == residues) & live_mask
    hit_hot = target_hot & (predicted == target)
    return jnp.stack(
        [
            jnp.sum(predicted_hot.astype(jnp.int32), 0),
            jnp.sum(target_hot.astype(jnp.int32), 0),
            jnp.sum(hit_hot.astype(jnp.int32), 0),
        ]
    )


def local(
    x_long,
    x_short,
    seg_long,
    seg_short,
    pred_long,
    target_long,
    pred_short,
    target_short,
    query_weight,
    key_weight,
    value_weight,
    out_weight,
    up_weight,
    down_weight,
    vectors,
    up_bias,
    grad_long,
    grad_short,
):
    long_rows = x_long.shape[0]
    local_len = x_long.shape[1]
    width = x_long.shape[2]
    short_rows = x_short.shape[0]
    short_len = x_short.shape[1]
    head_size = width // HEADS
    groups = lax.axis_size("seq")
    position = lax.axis_index("seq")
    seg_local = lax.dynamic_slice_in_dim(seg_long, position * local_len, local_len, 1)
    split = long_rows * local_len
    row_len = local_len * groups

    def long_heads(matrix, length):
        return matrix.reshape(long_rows, length, HEADS, head_size)

    def short_heads(matrix):
        return matrix.reshape(short_rows, short_len, HEADS, head_size)

    tokens = jnp.concatenate(
        [x_long.reshape(split, width), x_short.reshape(short_rows * short_len, width)], 0
    )
    queries = (project(tokens, query_weight) + vectors[0]).astype(jnp.bfloat16)
    key_rows = project(tokens, key_weight).astype(jnp.bfloat16)
    value_rows = (project(tokens, value_weight) + vectors[1]).astype(jnp.bfloat16)
    query_long = long_heads(queries[:split], local_len)
    local_pair = (
        key_rows[:split].reshape(long_rows, local_len, width),
        value_rows[:split].reshape(long_rows, local_len, width),
    )
    mixture_long, logsum_long = fold_attend(query_long, local_pair, seg_local, seg_long)
    query_short = short_heads(queries[split:])
    key_short = short_heads(key_rows[split:])
    value_short = short_heads(value_rows[split:])
    mixture_short, logsum_short = attend(query_short, key_short, value_short, seg_short, seg_short)
    mixture = jnp.concatenate(
        [mixture_long.reshape(split, width), mixture_short.reshape(-1, width)], 0
    ).astype(jnp.bfloat16)
    branch = project(mixture, out_weight) + vectors[2]
    hidden, normed_one, factor_one = normalize(
        tokens.astype(jnp.float32) + branch, vectors[4], vectors[5]
    )
    moved = lax.all_to_all(
        hidden[:split].reshape(long_rows, local_len, width),
        "seq",
        split_axis=0,
        concat_axis=1,
        tiled=True,
    )
    whole = jnp.concatenate([moved.reshape(split, width), hidden[split:]], 0)
    hidden_low = whole.astype(jnp.bfloat16)
    pre_act = project(hidden_low, up_weight) + up_bias
    activated, gelu_back = jax.vjp(lambda inner: jax.nn.gelu(inner, approximate=False), pre_act)
    act_low = activated.astype(jnp.bfloat16)
    output, normed_two, factor_two = normalize(
        whole + project(act_low, down_weight) + vectors[3], vectors[6], vectors[7]
    )
    out_long = output[:split].reshape(long_rows // groups, row_len, width)
    out_short = output[split:].reshape(short_rows, short_len, width)
    upstream = jnp.concatenate(
        [grad_long.reshape(split, width), grad_short.reshape(-1, width)], 0
    ).astype(jnp.float32)
    second_grad, gain_two, shift_two = normalize_back(upstream, normed_two, factor_two, vectors[6])
    down_in = second_grad.astype(jnp.bfloat16)
    down_grad = outer_sum(act_low, down_in)
    down_total = jnp.sum(down_in.astype(jnp.float32), 0)
    pre_grad = gelu_back(against(down_in, down_weight))[0].astype(jnp.bfloat16)
    up_grad = outer_sum(hidden_low, pre_grad)
    bias_total = jnp.sum(pre_grad.astype(jnp.float32), 0)
    whole_grad = second_grad + against(pre_grad, up_weight)
    returned = lax.all_to_all(
        whole_grad[:split].reshape(long_rows // groups, row_len, width),
        "seq",
        split_axis=1,
        concat_axis=0,
        tiled=True,
    )
    hidden_grad = jnp.concatenate([returned.reshape(split, width), whole_grad[split:]], 0)
    first_grad, gain_one, shift_one = normalize_back(
        hidden_grad, normed_one, factor_one, vectors[4]
    )
    branch_in = first_grad.astype(jnp.bfloat16)
    out_grad = outer_sum(mixture, branch_in)
    out_total = jnp.sum(branch_in.astype(jnp.float32), 0)
    mixture_grad = against(branch_in, out_weight).astype(jnp.bfloat16)
    keys_all, values_all = (
        lax.all_gather(local_pair[0], "seq", axis=1, tiled=True),
        lax.all_gather(local_pair[1], "seq", axis=1, tiled=True),
    )
    mixture_long_grad = mixture_grad[:split].reshape(long_rows, local_len, width)
    query_part, key_part, value_part = attend_back(
        query_long,
        long_heads(keys_all, row_len),
        long_heads(values_all, row_len),
        seg_local,
        seg_long,
        logsum_long,
        long_heads(mixture_long_grad, local_len),
    )
    key_back, value_back = (
        lax.psum_scatter(
            key_part.reshape(long_rows, row_len, width).astype(jnp.bfloat16),
            "seq",
            scatter_dimension=1,
            tiled=True,
        ).astype(jnp.float32),
        lax.psum_scatter(
            value_part.reshape(long_rows, row_len, width).astype(jnp.bfloat16),
            "seq",
            scatter_dimension=1,
            tiled=True,
        ).astype(jnp.float32),
    )
    query_small, key_small, value_small = attend_back(
        query_short,
        key_short,
        value_short,
        seg_short,
        seg_short,
        logsum_short,
        short_heads(mixture_grad[split:]),
    )
    query_in = jnp.concatenate(
        [query_part.reshape(split, width), query_small.reshape(-1, width)], 0
    ).astype(jnp.bfloat16)
    key_in = jnp.concatenate(
        [key_back.reshape(split, width), key_small.reshape(-1, width)], 0
    ).astype(jnp.bfloat16)
    value_in = jnp.concatenate(
        [value_back.reshape(split, width), value_small.reshape(-1, width)], 0
    ).astype(jnp.bfloat16)
    query_grad = outer_sum(tokens, query_in)
    key_grad = outer_sum(tokens, key_in)
    value_grad = outer_sum(tokens, value_in)
    token_grad = (
        first_grad
        + against(query_in, query_weight)
        + against(key_in, key_weight)
        + against(value_in, value_weight)
    )
    back_long = token_grad[:split].reshape(long_rows, local_len, width)
    back_short = token_grad[split:].reshape(short_rows, short_len, width)
    stacked = jnp.concatenate(
        [
            jnp.stack(
                [
                    jnp.sum(query_in.astype(jnp.float32), 0),
                    jnp.sum(value_in.astype(jnp.float32), 0),
                    out_total,
                    down_total,
                    gain_one,
                    shift_one,
                    gain_two,
                    shift_two,
                ]
            ),
            bias_total.reshape(-1, width),
        ],
        0,
    )
    members = (query_grad, key_grad, value_grad, out_grad, up_grad, down_grad, stacked)
    partial_sums = (
        lax.psum_scatter(
            members[0].astype(jnp.bfloat16), "seq", scatter_dimension=0, tiled=True
        ).astype(jnp.float32),
        lax.psum_scatter(
            members[1].astype(jnp.bfloat16), "seq", scatter_dimension=0, tiled=True
        ).astype(jnp.float32),
        lax.psum_scatter(
            members[2].astype(jnp.bfloat16), "seq", scatter_dimension=0, tiled=True
        ).astype(jnp.float32),
        lax.psum_scatter(
            members[3].astype(jnp.bfloat16), "seq", scatter_dimension=0, tiled=True
        ).astype(jnp.float32),
        lax.psum_scatter(
            members[4].astype(jnp.bfloat16), "seq", scatter_dimension=0, tiled=True
        ).astype(jnp.float32),
        lax.psum_scatter(
            members[5].astype(jnp.bfloat16), "seq", scatter_dimension=0, tiled=True
        ).astype(jnp.float32),
        lax.psum_scatter(
            members[6].astype(jnp.bfloat16), "seq", scatter_dimension=0, tiled=True
        ).astype(jnp.float32),
    )
    totals = lax.psum(
        (
            partial_sums[0],
            partial_sums[1],
            partial_sums[2],
            partial_sums[3],
            partial_sums[4],
            partial_sums[5],
            partial_sums[6],
        ),
        "dp",
    )
    summed = (
        lax.all_gather(totals[0].astype(jnp.bfloat16), "seq", axis=0, tiled=True).astype(
            jnp.float32
        ),
        lax.all_gather(totals[1].astype(jnp.bfloat16), "seq", axis=0, tiled=True).astype(
            jnp.float32
        ),
        lax.all_gather(totals[2].astype(jnp.bfloat16), "seq", axis=0, tiled=True).astype(
            jnp.float32
        ),
        lax.all_gather(totals[3].astype(jnp.bfloat16), "seq", axis=0, tiled=True).astype(
            jnp.float32
        ),
        lax.all_gather(totals[4].astype(jnp.bfloat16), "seq", axis=0, tiled=True).astype(
            jnp.float32
        ),
        lax.all_gather(totals[5].astype(jnp.bfloat16), "seq", axis=0, tiled=True).astype(
            jnp.float32
        ),
        lax.all_gather(totals[6].astype(jnp.bfloat16), "seq", axis=0, tiled=True).astype(
            jnp.float32
        ),
    )
    counts = tally(pred_long, target_long, seg_local) + tally(pred_short, target_short, seg_short)
    counts = lax.psum(counts, ("dp", "seq"))
    return (
        out_long,
        out_short,
        back_long,
        back_short,
        summed[0],
        summed[1],
        summed[2],
        summed[3],
        summed[4],
        summed[5],
        summed[6][:8],
        summed[6][8:].reshape(-1),
        counts,
    )


def solution(mesh):
    placed = (
        P("dp", "seq", None),
        P(("dp", "seq"), None, None),
        P("dp", None),
        P(("dp", "seq"), None),
        P("dp", "seq"),
        P("dp", "seq"),
        P(("dp", "seq"), None),
        P(("dp", "seq"), None),
        P(),
        P(),
        P(),
        P(),
        P(),
        P(),
        P(),
        P(),
        P(("dp", "seq"), None, None),
        P(("dp", "seq"), None, None),
    )
    return jax.shard_map(
        local,
        mesh=mesh,
        in_specs=placed,
        out_specs=(
            P(("dp", "seq"), None, None),
            P(("dp", "seq"), None, None),
            P("dp", "seq", None),
            P(("dp", "seq"), None, None),
            P(),
            P(),
            P(),
            P(),
            P(),
            P(),
            P(),
            P(),
            P(),
        ),
        check_vma=False,
    )
```

profile of v0, /device:TPU:0, one launch (start us, length us, event | category | flops | bytes accessed | tf_op | source)
XLA Modules:
  0.0 895.4 jit_solution(15918991827831710023)
XLA Ops:
  7.2 3.1 convolution_convert_fusion.3
  13.2 2.9 add_convert_fusion.1
  17.2 2.9 add_convert_fusion.2
  31.4 4.1 reshape.302
  35.5 3.5 copy.120
  39.2 2.5 select_reduce_fusion.1
  48.4 6.7 copy.119
  55.1 13.2 %select_reduce_fusion = (f32[4,12,160]{2,1,0:T(8,128)S(1)}, f32[4,12,160,640]{3,2,1,0:T(8,128)}) fusion(pred[4,160,640]{2,1,0:T(8,128)(4,1)S(1)} %broadcast_compare_fusion, bf16[4,160,12,64]{1,3,2,0:T(8,128)(2,1)S(1)} %copy.120, bf16[4,640,12,64]{1,3,2,0:T(8,128)(2,1)} %bitcast.101), kind=kOutput, calls=%fused_computation.4 | convolution fusion | flops 643883520 | bytes 25016320 | tf_op jit(solution)/shard_map/rqhe,rkhe->rhqk/dot_general | solution.py:54
  69.0 10.7 %fusion = f32[4,12,160]{2,1,0:T(8,128)S(1)} fusion(f32[4,12,160,640]{3,2,1,0:T(8,128)} %get-tuple-element.51, f32[4,12,160]{2,1,0:T(8,128)S(1)} %broadcast_maximum_fusion, pred[4,160,640]{2,1,0:T(8,128)(4,1)S(1)} %broadcast_compare_fusion), kind=kLoop, calls=%fused_computation.6 | loop fusion | flops 24568320 | bytes 20131840 | tf_op jit(solution)/shard_map/reduce_sum | solution.py:89
  79.6 3.9 all-gather.12.cloned.1.call-done
  83.5 6.2 copy.121
  89.8 10.5 %fusion.23 = bf16[4,160,12,64]{1,3,2,0:T(8,128)(2,1)S(1)} fusion(bf16[4,640,12,64]{1,3,2,0:T(8,128)(2,1)} %bitcast.105, f32[4,12,160,640]{3,2,1,0:T(8,128)} %get-tuple-element.51, f32[4,12,160]{2,1,0:T(8,128)S(1)} %broadcast_maximum_fusion, pred[4,160,640]{2,1,0:T(8,128)(4,1)S(1)} %broadcast_compare_fusion, f32[4,160,12]{1,2,0:T(8,128)S(1)} %bitcast.123), kind=kOutput, calls=%fused_computation.50 | convolution fusion | flops 649789440 | bytes 25047040 | tf_op jit(solution)/shard_map/rhqk,rkhe->rhqe/dot_general | solution.py:90
  110.5 3.9 all-to-all-start
  116.6 22.0 %all-to-all-done = f32[4,160,768]{2,1,0:T(8,128)S(1)} async-done(((f32[4,160,768]{2,1,0:T(8,128)}), f32[4,160,768]{2,1,0:T(8,128)S(1)}, u32[]{:S(2)}, u32[]{:S(2)}) %all-to-all-start) | async-done | bytes 1966112 | tf_op jit(solution)/shard_map/all_to_all | solution.py:202
  138.6 34.2 %multiply_convert_fusion.1 = (bf16[960,3072]{1,0:T(8,128)(2,1)S(1)}, f32[960,3072]{1,0:T(8,128)}, f32[960,3072]{1,0:T(8,128)}) fusion(f32[3072]{0:T(1024)S(1)} %copy-done.79, bf16[768,3072]{1,0:T(8,128)(2,1)} %param.30, f32[320,768]{1,0:T(8,128)} %slice.113, f32[640,768]{1,0:T(8,128)S(1)} %bitcast.117), kind=kOutput, calls=%fused_computation.10 | convolution fusion | flops 4727439360 | bytes 37171200 | tf_op jit(solution)/shard_map/dot_general | solution.py:15
  172.9 9.4 %fusion.89 = (f32[960]{0:T(1024)S(1)}, f32[960,768]{1,0:T(8,128)S(1)}) fusion(f32[768]{0:T(1024)S(1)} %copy-done.67, bf16[960,3072]{1,0:T(8,128)(2,1)S(1)} %get-tuple-element.45, bf16[3072,768]{1,0:T(8,128)(2,1)} %param.31, f32[320,768]{1,0:T(8,128)S(1)} %copy-done.38, f32[640,768]{1,0:T(8,128)S(1)} %bitcast.118), kind=kOutput, calls=%fused_computation.185 | convolution fusion | flops 4532796416 | bytes 16521984 | tf_op jit(solution)/shard_map/dot_general | solution.py:15
  183.6 4.5 fusion.27
  190.2 17.1 %fusion.93 = (bf16[3072]{0:T(1024)(128)(2,1)S(1)}, bf16[960,3072]{1,0:T(8,128)(2,1)}) fusion(f32[960,3072]{1,0:T(8,128)} %get-tuple-element.46, bf16[3072,768]{1,0:T(8,128)(2,1)} %param.31, f32[960,768]{1,0:T(8,128)S(1)} %get-tuple-element.42, f32[960,3072]{1,0:T(8,128)} %get-tuple-element.56, f32[3072]{0:T(1024)S(1)} %copy-done.79), kind=kOutput, calls=%fused_computation.189 | convolution fusion | flops 4577768448 | bytes 37177344 | tf_op jit(solution)/shard_map/dot_general | solution.py:25
  207.3 8.3 convolution_add_fusion
  217.3 3.3 copy.131
  220.6 3.7 all-to-all-start.1
  226.7 21.9 %all-to-all-done.1 = f32[1,640,768]{2,0,1:T(1,128)S(1)} async-done(((f32[1,640,768]{2,0,1:T(1,128)}), f32[1,640,768]{2,0,1:T(1,128)S(1)}, u32[]{:S(2)}, u32[]{:S(2)}) %all-to-all-start.1) | async-done | bytes 1966112 | tf_op jit(solution)/shard_map/all_to_all | solution.py:230
  257.3 2.6 reshape.306
  259.9 3.6 copy.133
  263.5 10.3 %fusion.29 = bf16[4,12,64,640]{3,2,1,0:T(8,128)(2,1)} fusion(bf16[4,160,12,64]{1,3,2,0:T(8,128)(2,1)S(1)} %copy.133, f32[4,12,160,640]{3,2,1,0:T(8,128)} %get-tuple-element.51, f32[4,12,160]{2,1,0:T(8,128)S(1)} %log_add_fusion, pred[4,160,640]{2,1,0:T(8,128)(4,1)S(1)} %copy-done.14), kind=kOutput, calls=%fused_computation.74 | convolution fusion | flops 645857280 | bytes 25016320 | tf_op jit(solution)/shard_map/rhqk,rqhe->rkhe/dot_general | solution.py:115
  273.8 6.3 copy.148
  280.2 16.2 %multiply_reduce_fusion = (f32[4,12,160]{2,1,0:T(8,128)S(1)}, f32[4,12,160,640]{3,2,1,0:T(8,128)}) fusion(f32[4,12,160,640]{3,2,1,0:T(8,128)} %get-tuple-element.51, f32[4,12,160]{2,1,0:T(8,128)S(1)} %log_add_fusion, pred[4,160,640]{2,1,0:T(8,128)(4,1)S(1)} %copy-done.14, bf16[4,160,12,64]{1,3,2,0:T(8,128)(2,1)S(1)} %copy.133, ...), kind=kOutput, calls=%fused_computation.1 | convolution fusion | flops 653713920 | bytes 44707840 | tf_op jit(solution)/shard_map/rqhe,rkhe->rhqk/dot_general | solution.py:101
  296.4 15.1 %multiply_convert_fusion = bf16[4,12,160,640]{3,2,1,0:T(8,128)(2,1)S(1)} fusion(f32[4,12,160,640]{3,2,1,0:T(8,128)} %get-tuple-element.62, f32[4,12,160,640]{3,2,1,0:T(8,128)} %get-tuple-element.51, f32[4,12,160]{2,1,0:T(8,128)S(1)} %get-tuple-element.61, f32[4,12,160]{2,1,0:T(8,128)S(1)} %log_add_fusion, pred[4,160,640]{2,1,0:T(8,128)(4,1)S(1)} %copy-done.14), kind=kLoop, calls=%fused_computation | loop fusion | flops 29491200 | bytes 49623040 | tf_op jit(solution)/shard_map/convert_element_type | solution.py:106
  311.5 3.7 multiply_convert_fusion.2
  316.4 6.3 copy.142
  325.6 5.0 convolution_convert_fusion.4
  330.7 3.8 multiply_reduce_fusion.1
  338.4 3.1 reshape.282
  341.5 9.7 %fusion.90 = (bf16[12,64]{1,0:T(8,128)(2,1)S(1)}, bf16[4,160,12,64]{1,3,2,0:T(8,128)(2,1)S(1)}) fusion(bf16[4,640,12,64]{1,3,2,0:T(8,128)(2,1)} %bitcast.102, bf16[4,12,160,640]{3,2,1,0:T(8,128)(2,1)} %copy-done.1), kind=kOutput, calls=%fused_computation.186 | convolution fusion | flops 630619392 | bytes 14747136 | tf_op jit(solution)/shard_map/rhqk,rkhe->rqhe/dot_general | solution.py:108
  353.6 3.9 reshape.280
  361.3 2.5 convolution_convert_fusion.7
  364.1 9.9 %convolution_convert_fusion.1 = bf16[768,3072]{1,0:T(8,128)(2,1)} fusion(bf16[960,3072]{1,0:T(8,128)(2,1)} %get-tuple-element.70, f32[320,768]{1,0:T(8,128)} %slice.113, f32[640,768]{1,0:T(8,128)} %bitcast.119), kind=kOutput, calls=%fused_computation.36 | convolution fusion | flops 4535156736 | bytes 13565952 | tf_op jit(solution)/shard_map/dot_general | solution.py:19
  374.1 9.5 %convolution_convert_fusion = bf16[3072,768]{1,0:T(8,128)(2,1)} fusion(bf16[960,3072]{1,0:T(8,128)(2,1)} %copy-done.81, f32[960,768]{1,0:T(8,128)} %copy-done.28), kind=kOutput, calls=%fused_computation.35 | convolution fusion | flops 4532944896 | bytes 13565952 | tf_op jit(solution)/shard_map/dot_general | solution.py:19
  383.7 4.3 fusion.92
  388.0 2.9 copy.158
  390.9 2.7 reshape.300
  393.6 4.3 convolution_convert_fusion.5
  398.4 2.8 fusion.52
  404.1 4.4 convolution_convert_fusion.6
  408.7 17.0 %reduce-scatter.13.cloned.1.call-done = bf16[192,768]{1,0:T(8,128)(2,1)} async-done(((bf16[768,768]{1,0:T(8,128)(2,1)}), bf16[192,768]{1,0:T(8,128)(2,1)}) %reduce-scatter.13.cloned.1.call-update) | async-done | bytes 294928 | tf_op jit(solution)/shard_map/reduce_scatter | solution.py:322
  425.6 50.5 %reduce-scatter.21.cloned.1.call-done = bf16[192,3072]{1,0:T(8,128)(2,1)} async-done(((bf16[768,3072]{1,0:T(8,128)(2,1)}), bf16[192,3072]{1,0:T(8,128)(2,1)}) %reduce-scatter.21.cloned.1.call-update) | async-done | bytes 1179664 | tf_op jit(solution)/shard_map/reduce_scatter | solution.py:334
  476.2 51.1 %reduce-scatter.23.cloned.1.call-done = bf16[768,768]{1,0:T(8,128)(2,1)} async-done(((bf16[3072,768]{1,0:T(8,128)(2,1)}), bf16[768,768]{1,0:T(8,128)(2,1)}) %reduce-scatter.23.cloned.1.call-update) | async-done | bytes 1179664 | tf_op jit(solution)/shard_map/reduce_scatter | solution.py:337
  527.3 28.8 %reduce-scatter.17.cloned.1.call-done = bf16[192,768]{1,0:T(8,128)(2,1)} async-done(((bf16[768,768]{1,0:T(8,128)(2,1)}), bf16[192,768]{1,0:T(8,128)(2,1)}) %reduce-scatter.17.cloned.1.call-update) | async-done | bytes 294928 | tf_op jit(solution)/shard_map/reduce_scatter | solution.py:328
  556.1 28.6 %reduce-scatter.15.cloned.1.call-done = bf16[192,768]{1,0:T(8,128)(2,1)} async-done(((bf16[768,768]{1,0:T(8,128)(2,1)}), bf16[192,768]{1,0:T(8,128)(2,1)}) %reduce-scatter.15.cloned.1.call-update) | async-done | bytes 294928 | tf_op jit(solution)/shard_map/reduce_scatter | solution.py:325
  584.9 143.3 %all-reduce.4.cloned.1.call-done = (bf16[192,768]{1,0:T(8,128)(2,1)}, bf16[192,768]{1,0:T(8,128)(2,1)}, bf16[192,768]{1,0:T(8,128)(2,1)}, bf16[192,768]{1,0:T(8,...) async-done(((bf16[192,768]{1,0:T(8,128)(2,1)}, bf16[192,768]{1,0:T(8,128)(2,1)}, bf16[192,768]{1,0:T(8,128)(2,1)}, bf16[192,768]{1,0:T(8,128)(2,1)}, ...) | async-done | bytes 3538960 | tf_op jit(solution)/shard_map/psum | solution.py:344
  733.8 39.5 %psum.63 = s32[3,24]{1,0:T(4,128)} all-reduce(s32[3,24]{1,0:T(4,128)S(1)} %add_add_fusion.3), channel_id=1, replica_groups=mesh['dp'=8,'seq'=4] {'dp','seq'}, use_global_device_ids=true, to_apply=%region_46.47 | all-reduce | flops 72 | bytes 576 | tf_op jit(solution)/shard_map/psum | solution.py:380
  775.7 2.9 slice_bitcast_fusion.1
  780.0 5.0 fusion.94
  785.3 10.6 %all-reduce = bf16[12,768]{1,0:T(8,128)(2,1)S(1)} all-reduce(bf16[12,768]{1,0:T(8,128)(2,1)S(1)} %concatenate.40), channel_id=10, replica_groups=mesh['dp'=8,'seq'=4] {'seq'}, use_global_device_ids=true, to_apply=%region_38.39.clone | all-reduce | flops 9216 | bytes 36864
  795.9 36.8 %psum.62 = bf16[3,768]{1,0:T(4,128)(2,1)S(1)} all-reduce(f32[3,768]{1,0:T(4,128)S(1)} %dynamic-slice_convert_fusion), channel_id=1, replica_groups=mesh['dp'=8,'seq'=4] {'dp'}, use_global_device_ids=true, to_apply=%region_39.40 | all-reduce | flops 2304 | bytes 13824 | tf_op jit(solution)/shard_map/psum | solution.py:344
  832.7 5.6 all-gather
  839.0 3.1 fusion.53
  847.3 2.8 convert_element_type.216
  850.1 3.0 convert_element_type.212
  853.1 2.9 convert_element_type.208
  856.1 2.8 convert_element_type.204
  858.9 6.8 convert_element_type.224
  865.7 15.6 %all-gather.22.cloned.1.call-done = bf16[768,3072]{1,0:T(8,128)(2,1)} async-done(((bf16[192,3072]{1,0:T(8,128)(2,1)}), bf16[768,3072]{1,0:T(8,128)(2,1)}) %all-gather.22.cloned.1.call-update) | async-done | bytes 4718608 | tf_op jit(solution)/shard_map/all_gather | solution.py:369
  881.3 7.4 convert_element_type.220
  (310 shorter events, 83.8 us)
Async XLA Ops:
  7.2 97.8 %copy-start = (bf16[768,768]{1,0:T(8,128)(2,1)S(1)}, bf16[768,768]{1,0:T(8,128)(2,1)}, u32[]{:S(2)}) copy-start(bf16[768,768]{1,0:T(8,128)(2,1)} %param.29) | copy-start | bytes 3538948
  7.2 41.2 %all-gather.10.cloned.1.call-start = ((), (), s32[]{:S(2)}) async-start(), calls=%async_computation.10 | async-start | bytes 4915200 | tf_op jit(solution)/shard_map/all_gather | solution.py:76
  12.5 71.0 %all-gather.12.cloned.1.call-start = ((), (), s32[]{:S(2)}) async-start(), calls=%async_computation.11 | async-start | bytes 4915200 | tf_op jit(solution)/shard_map/all_gather | solution.py:77
  13.2 94.0 %copy-start.54 = (f32[768]{0:T(1024)}, f32[768]{0:T(1024)S(1)}, u32[]{:S(2)}) copy-start(f32[768]{0:T(1024)S(1)} %get-tuple-element.22) | copy-start | bytes 9220
  16.1 4.0 copy-start.34
  27.7 11.6 %copy-start.18 = (bf16[2,160,12,64]{1,3,2,0:T(8,128)(2,1)}, bf16[2,160,12,64]{1,3,2,0:T(8,128)(2,1)S(1)}, u32[]{:S(2)}) copy-start(bf16[2,160,12,64]{1,3,2,0:T(8,128)(2,1)S(1)} %copy.126) | copy-start | bytes 1474564
  39.1 16.0 %copy-start.8 = (bf16[4,160,12,64]{1,3,2,0:T(8,128)(2,1)}, bf16[4,160,12,64]{1,3,2,0:T(8,128)(2,1)S(1)}, u32[]{:S(2)}) copy-start(bf16[4,160,12,64]{1,3,2,0:T(8,128)(2,1)S(1)} %copy.120) | copy-start | bytes 2949124
  39.2 3.6 copy-start.30
  47.9 41.9 %copy-start.13 = (pred[4,160,640]{2,1,0:T(8,128)(4,1)}, pred[4,160,640]{2,1,0:T(8,128)(4,1)S(1)}, u32[]{:S(2)}) copy-start(pred[4,160,640]{2,1,0:T(8,128)(4,1)S(1)} %broadcast_compare_fusion) | copy-start | bytes 1228804
  79.6 10.1 %copy-start.47 = (f32[4,12,160]{2,1,0:T(8,128)}, f32[4,12,160]{2,1,0:T(8,128)S(1)}, u32[]{:S(2)}) copy-start(f32[4,12,160]{2,1,0:T(8,128)S(1)} %fusion) | copy-start | bytes 92164
  110.5 28.1 %copy-start.79 = (f32[3072]{0:T(1024)S(1)}, f32[3072]{0:T(1024)}, u32[]{:S(2)}) copy-start(f32[3072]{0:T(1024)} %param.33) | copy-start | bytes 36868
  110.5 28.1 %all-to-all-start = ((f32[4,160,768]{2,1,0:T(8,128)}), f32[4,160,768]{2,1,0:T(8,128)S(1)}, u32[]{:S(2)}, u32[]{:S(2)}) async-start(f32[4,160,768]{2,1,0:T(8,128)} %bitcast.9), calls=%async_computation | async-start | bytes 3932160 | tf_op jit(solution)/shard_map/all_to_all | solution.py:202
  138.6 34.2 %copy-start.33 = (f32[4,160,768]{2,1,0:T(8,128)}, f32[4,160,768]{2,1,0:T(8,128)S(1)}, u32[]{:S(2)}) copy-start(f32[4,160,768]{2,1,0:T(8,128)S(1)} %all-to-all-done) | copy-start | bytes 5898244
  138.6 34.2 %copy-start.38 = (f32[320,768]{1,0:T(8,128)S(1)}, f32[320,768]{1,0:T(8,128)}, u32[]{:S(2)}) copy-start(f32[320,768]{1,0:T(8,128)} %slice.113) | copy-start | bytes 2949124
  138.6 34.2 %copy-start.67 = (f32[768]{0:T(1024)S(1)}, f32[768]{0:T(1024)}, u32[]{:S(2)}) copy-start(f32[768]{0:T(1024)} %get-tuple-element.20) | copy-start | bytes 9220
  172.8 9.5 %copy-start.81 = (bf16[960,3072]{1,0:T(8,128)(2,1)}, bf16[960,3072]{1,0:T(8,128)(2,1)S(1)}, u32[]{:S(2)}) copy-start(bf16[960,3072]{1,0:T(8,128)(2,1)S(1)} %get-tuple-element.45) | copy-start | bytes 17694724
  190.2 17.1 %copy-start.28 = (f32[960,768]{1,0:T(8,128)}, f32[960,768]{1,0:T(8,128)S(1)}, u32[]{:S(2)}) copy-start(f32[960,768]{1,0:T(8,128)S(1)} %get-tuple-element.42) | copy-start | bytes 8847364
  220.6 3.8 copy-start.42
  220.6 3.8 copy-start.48
  220.6 28.0 %all-to-all-start.1 = ((f32[1,640,768]{2,0,1:T(1,128)}), f32[1,640,768]{2,0,1:T(1,128)S(1)}, u32[]{:S(2)}, u32[]{:S(2)}) async-start(f32[1,640,768]{2,0,1:T(1,128)} %copy.131), calls=%async_computation.1 | async-start | bytes 3932160 | tf_op jit(solution)/shard_map/all_to_all | solution.py:230
  224.4 169.2 %reduce-scatter.11.cloned.1.call-start = ((), (), s32[]{:S(2)}) async-start(), calls=%async_computation.13 | async-start | bytes 4915200 | tf_op jit(solution)/shard_map/reduce_scatter | solution.py:266
  224.5 24.3 %copy-start.53 = (f32[960]{0:T(1024)S(1)}, f32[960]{0:T(1024)}, u32[]{:S(2)}) copy-start(f32[960]{0:T(1024)} %copy-done.52) | copy-start | bytes 11524
  224.5 24.3 %copy-start.55 = (f32[768]{0:T(1024)S(1)}, f32[768]{0:T(1024)}, u32[]{:S(2)}) copy-start(f32[768]{0:T(1024)} %copy-done.54) | copy-start | bytes 9220
  224.5 24.3 %copy-start.57 = (f32[960]{0:T(1024)S(1)}, f32[960]{0:T(1024)}, u32[]{:S(2)}) copy-start(f32[960]{0:T(1024)} %copy-done.56) | copy-start | bytes 11524
  248.6 4.1 copy-start.6
  280.1 124.0 %reduce-scatter.9.cloned.1.call-start = ((), (), s32[]{:S(2)}) async-start(), calls=%async_computation.12 | async-start | bytes 4915200 | tf_op jit(solution)/shard_map/reduce_scatter | solution.py:260
  296.4 15.1 %copy-start.9 = (bf16[4,160,12,64]{1,3,2,0:T(8,128)(2,1)S(1)}, bf16[4,160,12,64]{1,3,2,0:T(8,128)(2,1)}, u32[]{:S(2)}) copy-start(bf16[4,160,12,64]{1,3,2,0:T(8,128)(2,1)} %copy-done.8) | copy-start | bytes 2949124
  311.4 5.0 copy-start.1
  322.7 85.9 %reduce-scatter.19.cloned.1.call-start = ((), (), s32[]{:S(2)}) async-start(), calls=%async_computation.20 | async-start | bytes 1474560 | tf_op jit(solution)/shard_map/reduce_scatter | solution.py:331
  325.5 5.1 copy-start.25
  325.6 5.1 copy-start.24
  325.6 5.1 copy-start.31
  330.6 95.0 %reduce-scatter.13.cloned.1.call-start = ((), (), s32[]{:S(2)}) async-start(), calls=%async_computation.14 | async-start | bytes 1474560 | tf_op jit(solution)/shard_map/reduce_scatter | solution.py:322
  330.7 4.2 copy-start.3
  357.5 3.9 copy-start.75
  357.5 3.9 copy-start.78
  363.8 112.3 %reduce-scatter.21.cloned.1.call-start = ((), (), s32[]{:S(2)}) async-start(), calls=%async_computation.22 | async-start | bytes 5898240 | tf_op jit(solution)/shard_map/reduce_scatter | solution.py:334
  374.0 153.2 %reduce-scatter.23.cloned.1.call-start = ((), (), s32[]{:S(2)}) async-start(), calls=%async_computation.24 | async-start | bytes 5898240 | tf_op jit(solution)/shard_map/reduce_scatter | solution.py:337
  383.6 172.4 %reduce-scatter.17.cloned.1.call-start = ((), (), s32[]{:S(2)}) async-start(), calls=%async_computation.18 | async-start | bytes 1474560 | tf_op jit(solution)/shard_map/reduce_scatter | solution.py:328
  397.9 186.8 %reduce-scatter.15.cloned.1.call-start = ((), (), s32[]{:S(2)}) async-start(), calls=%async_computation.16 | async-start | bytes 1474560 | tf_op jit(solution)/shard_map/reduce_scatter | solution.py:325
  404.1 4.5 copy-start.43
  408.6 319.6 %all-reduce.4.cloned.1.call-start = ((), (), s32[]{:S(2)}) async-start(), calls=%async_computation.26 | async-start | bytes 7077888 | tf_op jit(solution)/shard_map/psum | solution.py:344
  584.7 146.6 %copy-start.17 = (bf16[1,640,768]{2,1,0:T(8,128)(2,1)S(1)}, bf16[1,640,768]{2,1,0:T(8,128)(2,1)}, u32[]{:S(2)}) copy-start(bf16[1,640,768]{2,1,0:T(8,128)(2,1)} %param.34) | copy-start | bytes 2949124
  584.7 146.8 %copy-start.21 = (bf16[2,160,768]{2,1,0:T(8,128)(2,1)S(1)}, bf16[2,160,768]{2,1,0:T(8,128)(2,1)}, u32[]{:S(2)}) copy-start(bf16[2,160,768]{2,1,0:T(8,128)(2,1)} %param.35) | copy-start | bytes 1474564
  584.8 146.9 %copy-start.62 = (s32[2,160]{1,0:T(2,128)S(1)}, s32[2,160]{1,0:T(2,128)}, u32[]{:S(2)}) copy-start(s32[2,160]{1,0:T(2,128)} %param.21) | copy-start | bytes 3844
  584.8 147.0 %copy-start.72 = (s32[2,160]{1,0:T(2,128)S(1)}, s32[2,160]{1,0:T(2,128)}, u32[]{:S(2)}) copy-start(s32[2,160]{1,0:T(2,128)} %param.24) | copy-start | bytes 3844
  584.8 147.1 %copy-start.73 = (s32[2,160]{1,0:T(2,128)S(1)}, s32[2,160]{1,0:T(2,128)}, u32[]{:S(2)}) copy-start(s32[2,160]{1,0:T(2,128)} %param.25) | copy-start | bytes 3844
  584.8 147.2 %copy-start.70 = (s32[4,160]{1,0:T(4,128)S(1)}, s32[4,160]{1,0:T(4,128)}, u32[]{:S(2)}) copy-start(s32[4,160]{1,0:T(4,128)} %param.22) | copy-start | bytes 7684
  584.8 147.2 %copy-start.71 = (s32[4,160]{1,0:T(4,128)S(1)}, s32[4,160]{1,0:T(4,128)}, u32[]{:S(2)}) copy-start(s32[4,160]{1,0:T(4,128)} %param.23) | copy-start | bytes 7684
  584.8 147.3 %copy-start.69 = (pred[4,160]{1,0:T(4,128)(4,1)S(1)}, pred[4,160]{1,0:T(4,128)(4,1)}, u32[]{:S(2)}) copy-start(pred[4,160]{1,0:T(4,128)(4,1)} %get-tuple-element.39) | copy-start | bytes 1924
  584.8 147.4 %copy-start.80 = (u32[32]{0:T(128)S(1)}, u32[32]{0:T(128)}, u32[]{:S(2)}) copy-start(u32[32]{0:T(128)} %constant.116) | copy-start | bytes 388
  584.8 188.5 %copy-start.65 = (bf16[768]{0:T(1024)(128)(2,1)S(1)}, bf16[768]{0:T(1024)(128)(2,1)}, u32[]{:S(2)}) copy-start(bf16[768]{0:T(1024)(128)(2,1)} %get-tuple-element.15) | copy-start | bytes 4612
  584.8 188.5 %copy-start.66 = (bf16[768]{0:T(1024)(128)(2,1)S(1)}, bf16[768]{0:T(1024)(128)(2,1)}, u32[]{:S(2)}) copy-start(bf16[768]{0:T(1024)(128)(2,1)} %get-tuple-element.41) | copy-start | bytes 4612
  584.9 262.4 %all-gather.20.cloned.1.call-start = ((), (), s32[]{:S(2)}) async-start(), calls=%async_computation.21 | async-start | bytes 1474560 | tf_op jit(solution)/shard_map/all_gather | solution.py:366
  728.3 121.9 %all-gather.18.cloned.1.call-start = ((), (), s32[]{:S(2)}) async-start(), calls=%async_computation.19 | async-start | bytes 1474560 | tf_op jit(solution)/shard_map/all_gather | solution.py:363
  729.0 124.1 %all-gather.16.cloned.1.call-start = ((), (), s32[]{:S(2)}) async-start(), calls=%async_computation.17 | async-start | bytes 1474560 | tf_op jit(solution)/shard_map/all_gather | solution.py:360
  729.6 126.5 %all-gather.14.cloned.1.call-start = ((), (), s32[]{:S(2)}) async-start(), calls=%async_computation.15 | async-start | bytes 1474560 | tf_op jit(solution)/shard_map/all_gather | solution.py:357
  730.2 128.7 %all-gather.24.cloned.1.call-start = ((), (), s32[]{:S(2)}) async-start(), calls=%async_computation.25 | async-start | bytes 5898240 | tf_op jit(solution)/shard_map/all_gather | solution.py:372
  730.7 150.6 %all-gather.22.cloned.1.call-start = ((), (), s32[]{:S(2)}) async-start(), calls=%async_computation.23 | async-start | bytes 5898240 | tf_op jit(solution)/shard_map/all_gather | solution.py:369
  773.3 5.3 copy-start.7
  780.0 5.0 copy-start.22
  780.0 59.0 %copy-start.44 = (bf16[320,768]{1,0:T(8,128)(2,1)S(1)}, bf16[320,768]{1,0:T(8,128)(2,1)}, u32[]{:S(2)}) copy-start(bf16[320,768]{1,0:T(8,128)(2,1)} %copy-done.43) | copy-start | bytes 1474564
  838.4 3.7 copy-start.49
  839.0 3.9 copy-start.37
  (40 other events, 77.3 us)
Sparse Core Ops, SparseCore 0:
  12.6 35.6 all-gather.9
  50.5 32.9 all-gather.11
  280.2 42.8 reduce-scatter.10
  325.5 42.8 reduce-scatter.8
  371.3 25.6 reduce-scatter.18
  400.0 25.6 reduce-scatter.12
  428.2 47.9 reduce-scatter.20
  479.3 47.9 reduce-scatter.22
  530.4 25.6 reduce-scatter.16
  559.1 25.6 reduce-scatter.14
  589.1 139.1 all-reduce.3
  729.6 16.8 all-gather.19
  748.1 17.4 all-gather.17
  767.0 17.4 all-gather.15
  785.9 17.5 all-gather.13
  804.9 37.5 all-gather.23
  843.8 37.4 all-gather.21
where the time goes:
time: 901 us; the launch traced here: 895 us
  waiting for transfers between devices  386 us (43%)
  matrix products  205 us (23%)
  local copies, waits for them, and re-layouts  116 us (13%)
  blocking collectives  92.5 us (10%)
  other arithmetic  70.3 us (8%)
  between operations  16.1 us (2%)
  starting transfers between devices  9.1 us (1%)
    psum x1, waiting for transfers between devices, local(): lax.psum((partial_sums[0], partial_sums[1], partial_sums[2], partial_sums...  143 us
    dot_general x6, matrix products, project(): return jnp.dot(matrix, weight, preferred_element_type=jnp.float32)  54.1 us
    reduce_scatter x1, waiting for transfers between devices, local(): lax.psum_scatter(members[5].astype(jnp.bfloat16), 'seq', scatter_dimensio...  51.1 us
    reduce_scatter x1, waiting for transfers between devices, local(): lax.psum_scatter(members[4].astype(jnp.bfloat16), 'seq', scatter_dimensio...  50.5 us
    psum x1, blocking collectives, local(): counts = lax.psum(counts, ('dp', 'seq'))  39.5 us
    psum x1, blocking collectives, local(): lax.psum((partial_sums[0], partial_sums[1], partial_sums[2], partial_sums...  36.8 us
    dot_general x6, matrix products, against(): lax.dot_general(matrix, weight, (((1,), (1,)), ((), ())), preferred_eleme...  36.1 us
    dot_general x6, matrix products, outer_sum(): lax.dot_general(first_op, second_op, (((0,), (0,)), ((), ())), preferred_...  35.6 us
  transfers between devices with their start and end apart: 19, of which 11 were waited for; matrix products, arithmetic and copies ran while one was open for 26% of the time, Pallas kernels for 0%

commit v1 on v0

v1 whole, which is shorter than its diff:
```python
import functools

import jax
import jax.numpy as jnp
from jax import lax
from jax.experimental import pallas as pl
from jax.experimental.pallas import tpu as pltpu
from jax.sharding import PartitionSpec as P

HEADS = 12
VOCAB = 24
LONG_REACH = 256

epsilon = 1e-05
blocked = -1e30


def project(matrix, weight):
    return jnp.dot(matrix, weight, preferred_element_type=jnp.float32)


def outer_sum(first_op, second_op):
    return lax.dot_general(
        first_op, second_op, (((0,), (0,)), ((), ())), preferred_element_type=jnp.float32
    )


def against(matrix, weight):
    return lax.dot_general(
        matrix, weight, (((1,), (1,)), ((), ())), preferred_element_type=jnp.float32
    )


def normalize(residual, gain_row, shift_row):
    centered = residual - jnp.mean(residual, -1, keepdims=True)
    factor = lax.rsqrt(jnp.mean(centered * centered, -1, keepdims=True) + epsilon)
    normed = centered * factor
    return (normed * gain_row + shift_row, normed, factor)


def normalize_back(upward, normed, factor, gain_row):
    scaled = upward * gain_row
    result = factor * (
        scaled
        - jnp.mean(scaled, -1, keepdims=True)
        - normed * jnp.mean(scaled * normed, -1, keepdims=True)
    )
    return (result, jnp.sum(upward * normed, 0), jnp.sum(upward, 0))


def blocks_of(long_len, short_len, short_rows):
    step = 128
    found = []
    for start in range(0, long_len, step):
        low = max(0, (start - LONG_REACH + 1) // step * step)
        high = min(long_len, -(-(start + step + LONG_REACH - 1) // step) * step)
        found.append((start, step, low, high, 0, 0))
    for row in range(short_rows):
        base = long_len + row * short_len
        found.append((base, short_len, base, base + short_len, base, row + 1))
    return found


def fill_bias(col_ref, row_ref, long_bias, short_bias, long_len, short_len, short_rows):
    col = col_ref[0:long_len, :]
    row = row_ref[0:1, 0:long_len]
    long_bias[...] = jnp.where(col == row, 0.0, blocked)
    for index in range(short_rows):
        base = long_len + index * short_len
        col = col_ref[base : base + short_len, :]
        row = row_ref[1 + index : 2 + index, 0:short_len]
        short_bias[index] = jnp.where(col == row, 0.0, blocked)


def bias_at(long_bias, short_bias, first, first_count, low, high, base, index):
    if index == 0:
        return long_bias[first : first + first_count, low:high]
    return short_bias[index - 1]


def two_heads(block, lanes, scale):
    half = block.shape[1] // 2
    zero = jnp.zeros_like(block)
    if scale != 1.0:
        block = block * scale
    return jnp.concatenate(
        [jnp.where(lanes < half, block, zero), jnp.where(lanes < half, zero, block)], 0
    )


def attend_kernel(sizes, scale, q_ref, k_ref, v_ref, col_ref, row_ref, o_ref, long_bias, short_bias):
    @pl.when(pl.program_id(0) == 0)
    def _():
        fill_bias(col_ref, row_ref, long_bias, short_bias, *sizes)

    for first, count, low, high, base, index in blocks_of(*sizes):
        lanes = lax.broadcasted_iota(jnp.int32, (count, 128), 1)
        pair = two_heads(q_ref[first : first + count, :], lanes, scale)
        scores = against(pair, k_ref[low:high, :])
        bias = bias_at(long_bias, short_bias, first, count, low, high, base, index)
        scores = scores + jnp.concatenate([bias, bias], 0)
        highest = jnp.max(scores, -1, keepdims=True)
        weights = jnp.exp(scores - highest)
        summed = jnp.sum(weights, -1, keepdims=True)
        mixed = project(weights.astype(jnp.bfloat16), v_ref[low:high, :]) / summed
        o_ref[first : first + count, :] = jnp.where(
            lanes < 64, mixed[:count], mixed[count:]
        ).astype(jnp.bfloat16)


def attend_back_kernel(
    sizes,
    scale,
    q_ref,
    k_ref,
    v_ref,
    g_ref,
    col_ref,
    row_ref,
    dq_ref,
    dk_ref,
    dv_ref,
    long_bias,
    short_bias,
    k_sum,
    v_sum,
):
    @pl.when(pl.program_id(0) == 0)
    def _():
        fill_bias(col_ref, row_ref, long_bias, short_bias, *sizes)

    k_sum[...] = jnp.zeros_like(k_sum)
    v_sum[...] = jnp.zeros_like(v_sum)
    for first, count, low, high, base, index in blocks_of(*sizes):
        lanes = lax.broadcasted_iota(jnp.int32, (count, 128), 1)
        pair = two_heads(q_ref[first : first + count, :], lanes, scale)
        upward = two_heads(g_ref[first : first + count, :], lanes, 1.0)
        keys = k_ref[low:high, :]
        scores = against(keys, pair)
        if index == 0:
            bias = long_bias[low:high, first : first + count]
        else:
            bias = short_bias[index - 1]
        scores = scores + jnp.concatenate([bias, bias], 1)
        highest = jnp.max(scores, 0, keepdims=True)
        weights = jnp.exp(scores - highest)
        weights = weights * (1.0 / jnp.sum(weights, 0, keepdims=True))
        weight_grad = against(v_ref[low:high, :], upward)
        delta = jnp.sum(weights * weight_grad, 0, keepdims=True)
        score_grad = (weights * (weight_grad - delta)).astype(jnp.bfloat16)
        v_sum[low:high, :] += project(weights.astype(jnp.bfloat16), upward)
        k_sum[low:high, :] += project(score_grad, pair)
        q_part = outer_sum(score_grad, keys) * scale
        dq_ref[first : first + count, :] = jnp.where(lanes < 64, q_part[:count], q_part[count:]).astype(
            jnp.bfloat16
        )
    dk_ref[...] = k_sum[...].astype(jnp.bfloat16)
    dv_ref[...] = v_sum[...].astype(jnp.bfloat16)


def attention_calls(sizes, rows, width, scale):
    long_len, short_len, short_rows = sizes
    pairs = width // 128
    column = pl.BlockSpec((rows, 128), lambda i: (0, i))
    col_spec = pl.BlockSpec((rows, 1), lambda i: (0, 0))
    row_spec = pl.BlockSpec((1 + short_rows, long_len), lambda i: (0, 0))
    shape = jax.ShapeDtypeStruct((rows, width), jnp.bfloat16)
    bias = [
        pltpu.VMEM((long_len, long_len), jnp.float32),
        pltpu.VMEM((short_rows, short_len, short_len), jnp.float32),
    ]
    forward = pl.pallas_call(
        functools.partial(attend_kernel, sizes, scale),
        grid=(pairs,),
        in_specs=[column] * 3 + [col_spec, row_spec],
        out_specs=column,
        out_shape=shape,
        scratch_shapes=bias,
        name="attend",
    )
    backward = pl.pallas_call(
        functools.partial(attend_back_kernel, sizes, scale),
        grid=(pairs,),
        in_specs=[column] * 4 + [col_spec, row_spec],
        out_specs=[column] * 3,
        out_shape=[shape] * 3,
        scratch_shapes=bias + [pltpu.VMEM((rows, 128), jnp.float32)] * 2,
        name="attend_back",
    )
    return forward, backward


def tally(predicted, target, segment):
    residues = jnp.arange(VOCAB, dtype=jnp.int32)[None, :]
    live_mask = (segment > 0).reshape(-1, 1)
    predicted = predicted.reshape(-1, 1)
    target = target.reshape(-1, 1)
    predicted_hot = (predicted == residues) & live_mask
    target_hot = (target == residues) & live_mask
    hit_hot = target_hot & (predicted == target)
    return jnp.stack(
        [
            jnp.sum(predicted_hot.astype(jnp.float32), 0),
            jnp.sum(target_hot.astype(jnp.float32), 0),
            jnp.sum(hit_hot.astype(jnp.float32), 0),
        ]
    )


def local(
    x_long,
    x_short,
    seg_long,
    seg_short,
    pred_long,
    target_long,
    pred_short,
    target_short,
    query_weight,
    key_weight,
    value_weight,
    out_weight,
    up_weight,
    down_weight,
    vectors,
    up_bias,
    grad_long,
    grad_short,
):
    local_len, width = x_long.shape[1:]
    short_rows, short_len = x_short.shape[:2]
    groups = lax.axis_size("seq")
    position = lax.axis_index("seq")
    row_len = local_len * groups
    rows_here = x_long.shape[0] // groups
    split = rows_here * row_len
    total = split + short_rows * short_len
    sizes = (row_len, short_len, short_rows)
    forward, backward = attention_calls(sizes, total, width, (width // HEADS) ** (-0.5))

    seg_row = lax.dynamic_slice_in_dim(seg_long, position * rows_here, rows_here, 0)
    seg_local = lax.dynamic_slice_in_dim(seg_long, position * local_len, local_len, 1)
    seg_rows = jnp.concatenate(
        [seg_row, jnp.pad(seg_short, ((0, 0), (0, row_len - short_len)), constant_values=-1)], 0
    )
    seg_column = jnp.concatenate([seg_row.reshape(-1, 1), seg_short.reshape(-1, 1)], 0)

    moved = lax.all_to_all(x_long, "seq", split_axis=0, concat_axis=1, tiled=True)
    tokens = jnp.concatenate([moved.reshape(split, width), x_short.reshape(-1, width)], 0)
    queries = (project(tokens, query_weight) + vectors[0]).astype(jnp.bfloat16)
    key_rows = project(tokens, key_weight).astype(jnp.bfloat16)
    value_rows = (project(tokens, value_weight) + vectors[1]).astype(jnp.bfloat16)
    mixture = forward(queries, key_rows, value_rows, seg_column, seg_rows)
    branch = project(mixture, out_weight) + vectors[2]
    hidden, normed_one, factor_one = normalize(
        tokens.astype(jnp.float32) + branch, vectors[4], vectors[5]
    )
    hidden_low = hidden.astype(jnp.bfloat16)
    pre_act = project(hidden_low, up_weight) + up_bias
    activated, gelu_back = jax.vjp(lambda inner: jax.nn.gelu(inner, approximate=False), pre_act)
    act_low = activated.astype(jnp.bfloat16)
    output, normed_two, factor_two = normalize(
        hidden + project(act_low, down_weight) + vectors[3], vectors[6], vectors[7]
    )
    out_long = output[:split].reshape(rows_here, row_len, width)
    out_short = output[split:].reshape(short_rows, short_len, width)
    upstream = jnp.concatenate(
        [grad_long.reshape(split, width), grad_short.reshape(-1, width)], 0
    ).astype(jnp.float32)
    second_grad, gain_two, shift_two = normalize_back(upstream, normed_two, factor_two, vectors[6])
    down_in = second_grad.astype(jnp.bfloat16)
    down_grad = outer_sum(act_low, down_in)
    down_total = jnp.sum(down_in.astype(jnp.float32), 0)
    pre_grad = gelu_back(against(down_in, down_weight))[0].astype(jnp.bfloat16)
    up_grad = outer_sum(hidden_low, pre_grad)
    bias_total = jnp.sum(pre_grad.astype(jnp.float32), 0)
    hidden_grad = second_grad + against(pre_grad, up_weight)
    first_grad, gain_one, shift_one = normalize_back(
        hidden_grad, normed_one, factor_one, vectors[4]
    )
    branch_in = first_grad.astype(jnp.bfloat16)
    out_grad = outer_sum(mixture, branch_in)
    out_total = jnp.sum(branch_in.astype(jnp.float32), 0)
    mixture_grad = against(branch_in, out_weight).astype(jnp.bfloat16)
    query_in, key_in, value_in = backward(
        queries, key_rows, value_rows, mixture_grad, seg_column, seg_rows
    )
    query_grad = outer_sum(tokens, query_in)
    key_grad = outer_sum(tokens, key_in)
    value_grad = outer_sum(tokens, value_in)
    token_grad = (
        first_grad
        + against(query_in, query_weight)
        + against(key_in, key_weight)
        + against(value_in, value_weight)
    )
    returned = lax.all_to_all(
        token_grad[:split].reshape(rows_here, row_len, width).astype(jnp.bfloat16),
        "seq",
        split_axis=1,
        concat_axis=0,
        tiled=True,
    )
    back_long = returned.astype(jnp.float32)
    back_short = token_grad[split:].reshape(short_rows, short_len, width)
    counts = tally(pred_long, target_long, seg_local) + tally(pred_short, target_short, seg_short)
    small = jnp.concatenate(
        [
            jnp.stack(
                [
                    jnp.sum(query_in.astype(jnp.float32), 0),
                    jnp.sum(value_in.astype(jnp.float32), 0),
                    out_total,
                    down_total,
                    gain_one,
                    shift_one,
                    gain_two,
                    shift_two,
                ]
            ),
            bias_total.reshape(-1, width),
            jnp.pad(counts.reshape(1, -1), ((0, 0), (0, width - counts.size))),
        ],
        0,
    )
    members = tuple(
        part.astype(jnp.bfloat16)
        for part in (query_grad, key_grad, value_grad, out_grad, up_grad, down_grad)
    )
    summed = lax.psum(members, ("dp", "seq"))
    small = lax.psum(small, ("dp", "seq"))
    return (
        out_long,
        out_short,
        back_long,
        back_short,
        *(part.astype(jnp.float32) for part in summed),
        small[:8],
        small[8:-1].reshape(-1),
        small[-1, : counts.size].reshape(counts.shape).astype(jnp.int32),
    )


def solution(mesh):
    placed = (
        P("dp", "seq", None),
        P(("dp", "seq"), None, None),
        P("dp", None),
        P(("dp", "seq"), None),
        P("dp", "seq"),
        P("dp", "seq"),
        P(("dp", "seq"), None),
        P(("dp", "seq"), None),
        P(),
        P(),
        P(),
        P(),
        P(),
        P(),
        P(),
        P(),
        P(("dp", "seq"), None, None),
        P(("dp", "seq"), None, None),
    )
    return jax.shard_map(
        local,
        mesh=mesh,
        in_specs=placed,
        out_specs=(
            P(("dp", "seq"), None, None),
            P(("dp", "seq"), None, None),
            P("dp", "seq", None),
            P(("dp", "seq"), None, None),
            P(),
            P(),
            P(),
            P(),
            P(),
            P(),
            P(),
            P(),
            P(),
        ),
        check_vma=False,
    )
```

time: 901 us -> 474 us (0.53)
  waiting for transfers between devices: 386 us -> 166 us
  matrix products: 205 us -> 114 us
  local copies, waits for them, and re-layouts: 116 us -> 28.4 us
  Pallas kernels: 0 us -> 43.4 us
  blocking collectives: 92.5 us -> 52.1 us
  other arithmetic: 70.3 us -> 38.1 us
    reduce_scatter x8 -> x0, waiting for transfers between devices: 176 us -> none  [the longest x1 51.1 us: local(): lax.psum_scatter(members[5].astype(jnp.bfloat16), 'seq', scatter_dimensio...]
    dot_general x12 -> x0, matrix products: 78.8 us -> none  [the longest x2 19.9 us: attend_back(): jnp.einsum('rqhe,rkhe->rhqk', mixture_grad, values_in, preferred_element_...]
    pallas_call x0 -> x2, Pallas kernels: none -> 43.4 us  [the longest x1 26.7 us: local(): backward(queries, key_rows, value_rows, mixture_grad, seg_column, seg_rows)]
    reshape x22 -> x4, local copies, waits for them, and re-layouts: 43.2 us -> 5.02 us  [the longest x1 2.94 us: local(): out_long = output[:split].reshape(rows_here, row_len, width)]
    all_to_all x2, waiting for transfers between devices: 43.9 us -> 8.15 us  [the longest x1 8.15 us: local(): lax.all_to_all(x_long, 'seq', split_axis=0, concat_axis=1, tiled=True)]
    psum x2 -> x1, blocking collectives: 76.3 us -> 52.1 us  [local(): small = lax.psum(small, ('dp', 'seq'))]
    convert_element_type x9 -> x7, other arithmetic: 42.2 us -> 18.3 us  [the longest x6 18.3 us: local(): part.astype(jnp.float32)]
    all_gather x8 -> x0, waiting for transfers between devices: 19.9 us -> none  [the longest x1 15.6 us: local(): lax.all_gather(totals[4].astype(jnp.bfloat16), 'seq', axis=0, tiled=True)]
  transfers between devices with their start and end apart: 19 -> 3, of which waited for: 11 -> 2; matrix products, arithmetic and copies ran while one was open for 26% -> 9% of each run, Pallas kernels for 0% -> 0%
where the time goes in v1:
time: 474 us; the launch traced here: 465 us
  waiting for transfers between devices  166 us (35%)
  matrix products  114 us (24%)
  blocking collectives  52.1 us (11%)
  Pallas kernels  43.4 us (9%)
  other arithmetic  38.1 us (8%)
  local copies, waits for them, and re-layouts  28.4 us (6%)
  between operations  14.9 us (3%)
  starting transfers between devices  8.63 us (2%)
    psum x1, waiting for transfers between devices, local(): summed = lax.psum(members, ('dp', 'seq'))  158 us
    psum x1, blocking collectives, local(): small = lax.psum(small, ('dp', 'seq'))  52.1 us
    dot_general x6, matrix products, project(): return jnp.dot(matrix, weight, preferred_element_type=jnp.float32)  50.6 us
    dot_general x6, matrix products, against(): lax.dot_general(matrix, weight, (((1,), (1,)), ((), ())), preferred_eleme...  36.8 us
    pallas_call x1, Pallas kernels, local(): backward(queries, key_rows, value_rows, mixture_grad, seg_column, seg_rows)  26.7 us
    dot_general x6, matrix products, outer_sum(): lax.dot_general(first_op, second_op, (((0,), (0,)), ((), ())), preferred_...  26.3 us
    convert_element_type x6, other arithmetic, local(): part.astype(jnp.float32)  18.3 us
    pallas_call x1, Pallas kernels, local(): mixture = forward(queries, key_rows, value_rows, seg_column, seg_rows)  16.7 us
  transfers between devices with their start and end apart: 3, of which 2 were waited for; matrix products, arithmetic and copies ran while one was open for 9% of the time, Pallas kernels for 0%

profile of v1, /device:TPU:0, one launch (start us, length us, event | category | flops | bytes accessed | tf_op | source)
XLA Modules:
  0.0 465.0 jit_solution(2796990822834652833)
XLA Ops:
  7.2 4.4 all-to-all-start
  11.6 0.8 reshape.170
  12.4 0.7 fusion.62
  13.1 1.0 copy.36.col_ref
  14.1 0.7 constant_dynamic-slice_fusion
  14.8 1.3 select_add_fusion.row_ref
  16.1 1.1 slice_reduce_fusion.1
  17.2 8.1 %all-to-all-done = bf16[4,160,768]{2,1,0:T(8,128)(2,1)S(1)} async-done(((bf16[4,160,768]{2,1,0:T(8,128)(2,1)}), bf16[4,160,768]{2,1,0:T(8,128)(2,1)S(1)}, u32[]{:S(2)}, u32[]{:S(2)}) %all-to-all-start) | async-done | bytes 983072 | tf_op jit(solution)/shard_map/all_to_all | solution.py:248
  25.3 4.2 convolution_convert_fusion.3.k_ref
  29.6 2.4 add_convert_fusion.1.v_ref
  32.0 2.4 add_convert_fusion.2.q_ref
  34.5 16.7 %attend.1 = bf16[960,768]{1,0:T(8,128)(2,1)} custom-call(bf16[960,768]{1,0:T(8,128)(2,1)} %add_convert_fusion.2.q_ref, bf16[960,768]{1,0:T(8,128)(2,1)} %convolution_convert_fusion.3.k_ref, bf16[960,768]{1,0:T(8,128)(2,1)} %add_convert_fusion.1.v_ref, s32[960,1]{1,0:T(8,128)} %copy.36.col_ref, s32[3,640]{1,0:T(4,128)} %select_add_fusion.row_ref), custom_call_target="tpu_custom_call" | custom-call | tf_op jit(solution)/shard_map/attend/pallas_call | solution.py:253
  51.2 3.0 fusion.34
  54.2 0.5 multiply_reduce_fusion.3
  54.7 0.2 copy-done.32
  54.9 33.3 %multiply_convert_fusion = (bf16[960,3072]{1,0:T(8,128)(2,1)S(1)}, f32[960,3072]{1,0:T(8,128)}, f32[960,3072]{1,0:T(8,128)}) fusion(f32[3072]{0:T(1024)S(1)} %copy-done.32, bf16[768,3072]{1,0:T(8,128)(2,1)S(1)} %bitcast.72, f32[960,768]{1,0:T(8,128)S(1)} %get-tuple-element.55, f32[768]{0:T(1024)S(1)} %get-tuple-element.29, f32[768]{0:T(1024)S(1)} %get-tuple-element.30, ...), kind=kOutput, calls=%fused_computation.4 | convolution fusion | flops 4728176640 | bytes 37185024 | tf_op jit(solution)/shard_map/dot_general | solution.py:19
  88.2 5.1 %fusion.35 = (f32[960]{0:T(1024)S(1)}, f32[960,768]{1,0:T(8,128)S(1)}) fusion(f32[768]{0:T(1024)S(1)} %get-tuple-element.28, bf16[960,3072]{1,0:T(8,128)(2,1)S(1)} %get-tuple-element.51, bf16[3072,768]{1,0:T(8,128)(2,1)S(1)} %bitcast.70, f32[768]{0:T(1024)S(1)} %get-tuple-element.29, f32[768]{0:T(1024)S(1)} %get-tuple-element.30, ...), kind=kOutput, calls=%fused_computation.110 | convolution fusion | flops 4535008256 | bytes 16535808 | tf_op jit(solution)/shard_map/dot_general | solution.py:19
  93.4 0.5 multiply_reduce_fusion.2
  93.9 0.7 copy-done.7
  94.7 2.4 fusion.12
  97.1 3.0 convert_reduce_fusion.2
  100.1 7.0 %convolution_convert_fusion = bf16[3072,768]{1,0:T(8,128)(2,1)} fusion(bf16[960,3072]{1,0:T(8,128)(2,1)S(1)} %get-tuple-element.51, f32[960,768]{1,0:T(8,128)S(1)} %get-tuple-element.48), kind=kOutput, calls=%fused_computation.18 | convolution fusion | flops 4532944896 | bytes 13565952 | tf_op jit(solution)/shard_map/dot_general | solution.py:23
  107.1 18.1 %convert_reduce_fusion = (f32[3072]{0:T(1024)S(1)}, bf16[960,3072]{1,0:T(8,128)(2,1)}) fusion(f32[960,3072]{1,0:T(8,128)} %get-tuple-element.52, bf16[3072,768]{1,0:T(8,128)(2,1)} %param.31, f32[960,768]{1,0:T(8,128)} %copy-done.8, f32[960,3072]{1,0:T(8,128)} %get-tuple-element.56, f32[3072]{0:T(1024)S(1)} %copy-done.32), kind=kOutput, calls=%fused_computation.2 | convolution fusion | flops 4580717568 | bytes 37183488 | tf_op jit(solution)/shard_map/dot_general | solution.py:29
  125.2 10.7 %multiply_reduce_fusion = (f32[768]{0:T(1024)S(1)}, f32[960]{0:T(1024)S(1)}, f32[960]{0:T(1024)S(1)}, f32[768]{0:T(1024)S(1)}, f32[960,768]{1,0:T(8,128)S(1)}) fusion(f32[960,768]{1,0:T(8,128)S(1)} %get-tuple-element.55, f32[960]{0:T(1024)S(1)} %add_rsqrt_fusion.1, f32[960]{0:T(1024)S(1)} %broadcast_multiply_fusion.5, f32[768]{0:T(1024)S(1)} %get-tuple-element.30, ...), kind=kOutput, calls=%fused_computation.30 | convolution fusion | flops 4537217024 | bytes 19488768 | tf_op jit(solution)/shard_map/dot_general | solution.py:29
  135.9 7.9 %convolution_convert_fusion.1 = bf16[768,3072]{1,0:T(8,128)(2,1)} fusion(bf16[960,3072]{1,0:T(8,128)(2,1)S(1)} %copy-done.33, f32[960,768]{1,0:T(8,128)S(1)} %get-tuple-element.55, f32[768]{0:T(1024)S(1)} %get-tuple-element.29, f32[768]{0:T(1024)S(1)} %get-tuple-element.30, f32[960]{0:T(1024)S(1)} %add_rsqrt_fusion.1, f32[960]{0:T(1024)S(1)} %broadcast_multiply_fusion.5), kind=kOutput, calls=%fused_computation.19 | convolution fusion | flops 4535894016 | bytes 13579776 | tf_op jit(solution)/shard_map/dot_general | solution.py:23
  143.8 1.2 convert_reduce_fusion.3
  145.1 2.5 convolution_convert_fusion.2.g_ref
  147.6 2.5 convolution_convert_fusion.4
  150.1 26.7 %attend_back.1 = (bf16[960,768]{1,0:T(8,128)(2,1)}, bf16[960,768]{1,0:T(8,128)(2,1)}, bf16[960,768]{1,0:T(8,128)(2,1)}) custom-call(bf16[960,768]{1,0:T(8,128)(2,1)} %add_convert_fusion.2.q_ref, bf16[960,768]{1,0:T(8,128)(2,1)} %convolution_convert_fusion.3.k_ref, bf16[960,768]{1,0:T(8,128)(2,1)} %add_convert_fusion.1.v_ref, ...), custom_call_target="tpu_custom_call" | custom-call | tf_op jit(solution)/shard_map/attend_back/pallas_call | solution.py:285
  176.9 4.0 convolution_convert_fusion.5
  180.9 2.5 convolution_convert_fusion.6
  183.3 2.5 convolution_convert_fusion.7
  185.8 0.8 dynamic-slice_compare_fusion
  187.3 0.2 convert_reduce_fusion.7
  187.6 2.8 fusion.36
  190.4 1.3 fusion.37
  191.8 0.5 copy-done.2
  192.2 0.6 copy-done.4
  192.8 0.7 copy-done.13
  193.5 1.3 add_add_fusion
  194.8 1.5 copy-done.3
  196.5 1.5 copy.41
  198.0 0.5 broadcast.115
  198.5 7.8 %reduce.20 = bf16[640,768]{1,0:T(8,128)(2,1)} reduce(bf16[640,1,768]{2,1,0:T(2,128)(2,1)S(1)} %bitcast.47, bf16[]{:T(256)} %broadcast.115), dimensions={1}, to_apply=%bitcast.46.reduce_sub_computation | reduce | bytes 1966082
  206.3 3.6 reshape.194
  209.9 4.2 all-to-all-start.1
  214.1 1.7 convert_reduce_fusion.5
  215.8 0.3 convert_reduce_fusion.4
  216.2 52.1 %psum.55 = f32[13,768]{1,0:T(8,128)S(1)} all-reduce(f32[13,768]{1,0:T(8,128)S(1)} %concatenate.19), channel_id=1, replica_groups=mesh['dp'=8,'seq'=4] {'dp','seq'}, use_global_device_ids=true, to_apply=%region_29.30 | all-reduce | flops 9984 | bytes 79872 | tf_op jit(solution)/shard_map/psum | solution.py:331
  268.3 0.6 slice.67
  268.9 2.2 slice.66
  271.1 0.6 reshape.177
  271.8 0.7 convert_element_type.158
  272.4 2.2 slice.64
  274.7 2.9 slice_bitcast_fusion
  277.6 2.6 reshape.195
  280.2 1.4 copy.39
  281.6 157.7 %all-reduce.5.cloned.1.call-done = (bf16[768,768]{1,0:T(8,128)(2,1)}, bf16[768,768]{1,0:T(8,128)(2,1)}, bf16[768,768]{1,0:T(8,128)(2,1)}, bf16[768,768]{1,0:T(8,...) async-done(((bf16[768,768]{1,0:T(8,128)(2,1)}, bf16[768,768]{1,0:T(8,128)(2,1)}, bf16[768,768]{1,0:T(8,128)(2,1)}, bf16[768,768]{1,0:T(8,128)(2,1)}, ...) | async-done | bytes 14155792 | tf_op jit(solution)/shard_map/psum | solution.py:330
  439.3 7.5 %convert_element_type.143 = f32[768,3072]{1,0:T(8,128)} convert(bf16[768,3072]{1,0:T(8,128)(2,1)} %get-tuple-element.45) | non-fusion elementwise | flops 2359296 | bytes 14155776 | tf_op jit(solution)/shard_map/convert_element_type | solution.py:337
  446.9 4.5 convert_element_type.145
  451.4 1.6 convert_element_type.135
  453.0 1.6 convert_element_type.137
  454.6 1.6 convert_element_type.139
  456.2 1.6 convert_element_type.141
  (109 shorter events, 1.5 us)
Async XLA Ops:
  7.2 44.0 %copy-start = (bf16[768,768]{1,0:T(8,128)(2,1)S(1)}, bf16[768,768]{1,0:T(8,128)(2,1)}, u32[]{:S(2)}) copy-start(bf16[768,768]{1,0:T(8,128)(2,1)} %param.29) | copy-start | bytes 3538948
  7.2 18.1 %all-to-all-start = ((bf16[4,160,768]{2,1,0:T(8,128)(2,1)}), bf16[4,160,768]{2,1,0:T(8,128)(2,1)S(1)}, u32[]{:S(2)}, u32[]{:S(2)}) async-start(bf16[4,160,768]{2,1,0:T(8,128)(2,1)} %param.18), calls=%async_computation | async-start | bytes 1966080 | tf_op jit(solution)/shard_map/all_to_all | solution.py:248
  11.6 427.7 %all-reduce.5.cloned.1.call-start = ((), (), s32[]{:S(2)}) async-start(), calls=%async_computation.2 | async-start | bytes 28311552 | tf_op jit(solution)/shard_map/psum | solution.py:330
  25.3 25.8 %copy-start.18 = (bf16[4,160,768]{2,1,0:T(8,128)(2,1)}, bf16[4,160,768]{2,1,0:T(8,128)(2,1)S(1)}, u32[]{:S(2)}) copy-start(bf16[4,160,768]{2,1,0:T(8,128)(2,1)S(1)} %all-to-all-done) | copy-start | bytes 2949124
  25.3 4.2 copy-start.12
  25.3 4.2 copy-start.30
  29.6 2.4 copy-start.28
  51.1 3.6 slice-start.2
  51.1 3.6 slice-start.3
  51.1 37.1 %slice-start = ((s8[4718592]{0:T(1024)(128)(4,1)}), s8[4194304]{0:T(1024)(128)(4,1)S(1)}, s32[]{:S(2)}) async-start(s8[4718592]{0:T(1024)(128)(4,1)} %bitcast.69), calls=%async_computation.3 | async-start | bytes 8388608
  54.2 0.7 copy-start.32
  54.9 33.3 %slice-start.1 = ((s8[4718592]{0:T(1024)(128)(4,1)}), s8[524288]{0:T(1024)(128)(4,1)S(1)}, s32[]{:S(2)}) async-start(s8[4718592]{0:T(1024)(128)(4,1)} %bitcast.69), calls=%async_computation.4 | async-start | bytes 1048576
  93.4 1.2 copy-start.7
  93.4 1.3 copy-start.9
  100.1 7.0 %copy-start.8 = (f32[960,768]{1,0:T(8,128)}, f32[960,768]{1,0:T(8,128)S(1)}, u32[]{:S(2)}) copy-start(f32[960,768]{1,0:T(8,128)S(1)} %get-tuple-element.48) | copy-start | bytes 8847364
  125.2 10.7 %copy-start.33 = (bf16[960,3072]{1,0:T(8,128)(2,1)S(1)}, bf16[960,3072]{1,0:T(8,128)(2,1)}, u32[]{:S(2)}) copy-start(bf16[960,3072]{1,0:T(8,128)(2,1)} %get-tuple-element.61) | copy-start | bytes 17694724
  145.1 2.5 copy-start.1
  145.1 2.5 copy-start.11
  150.1 26.7 %copy-start.19 = (bf16[4,160,768]{2,1,0:T(8,128)(2,1)S(1)}, bf16[4,160,768]{2,1,0:T(8,128)(2,1)}, u32[]{:S(2)}) copy-start(bf16[4,160,768]{2,1,0:T(8,128)(2,1)} %copy-done.18) | copy-start | bytes 2949124
  150.1 26.7 %copy-start.31 = (bf16[2,160,768]{2,1,0:T(8,128)(2,1)S(1)}, bf16[2,160,768]{2,1,0:T(8,128)(2,1)}, u32[]{:S(2)}) copy-start(bf16[2,160,768]{2,1,0:T(8,128)(2,1)} %param.19) | copy-start | bytes 1474564
  176.8 4.0 copy-start.20
  176.9 4.0 copy-start.26
  180.9 2.5 copy-start.10
  185.8 0.9 copy-start.22
  185.8 1.0 copy-start.23
  185.8 1.1 copy-start.24
  185.8 1.2 copy-start.25
  185.8 1.3 copy-start.21
  187.6 2.8 copy-start.27
  187.6 2.8 copy-start.29
  190.4 1.8 copy-start.2
  190.4 2.4 copy-start.4
  190.4 3.1 copy-start.13
  194.8 1.6 copy-start.3
  206.3 9.5 %copy-start.5 = (bf16[960,768]{1,0:T(8,128)(2,1)S(1)}, bf16[960,768]{1,0:T(8,128)(2,1)}, u32[]{:S(2)}) copy-start(bf16[960,768]{1,0:T(8,128)(2,1)} %get-tuple-element.18) | copy-start | bytes 4423684
  209.9 67.7 %all-to-all-start.1 = ((bf16[4,2,61440]{2,1,0:T(2,128)(2,1)}), bf16[4,2,61440]{2,1,0:T(2,128)(2,1)}, u32[]{:S(2)}, u32[]{:S(2)}) async-start(bf16[4,2,61440]{2,1,0:T(2,128)(2,1)} %reshape.194), calls=%async_computation.1 | async-start | bytes 1966080 | tf_op jit(solution)/shard_map/all_to_all | solution.py:297
  439.3 7.5 %copy-start.6 = (bf16[3072,768]{1,0:T(8,128)(2,1)S(1)}, bf16[3072,768]{1,0:T(8,128)(2,1)}, u32[]{:S(2)}) copy-start(bf16[3072,768]{1,0:T(8,128)(2,1)} %get-tuple-element.46) | copy-start | bytes 14155780
  446.9 4.5 copy-start.17
  451.3 1.7 copy-start.16
  451.4 3.2 copy-start.15
  453.0 3.2 copy-start.14
Sparse Core Ops, SparseCore 0:
  186.0 253.3 all-reduce.4
